TPU v7x, 32 devices: a whole 2x2x4 slice. The times are simulated.
32 devices in a mesh: heads: 2 (over x), seq: 16 (over z, y, core).
Axes of the slice: x: 2, y: 2, z: 4, core: 2. Of those that a mesh axis runs over, the one named last changes fastest.
Arguments:
- q_nope: bfloat16 [1152, 64, 128], P('seq', 'heads'), may hold values from -6 to 6
- q_rope: bfloat16 [1152, 64, 64], P('seq', 'heads'), may hold values from -125 to 125
- latent: bfloat16 [1152, 512], P('seq'), may hold values from -6 to 6
- key_rope: bfloat16 [1152, 64], P('seq'), may hold values from -5 to 5
- absorb_key: bfloat16 [64, 128, 512], P('heads'), may hold values from -0.5 to 0.5
- absorb_value: bfloat16 [64, 512, 128], P('heads'), may hold values from -0.25 to 0.25
- w_out: bfloat16 [8192, 3584], P('heads', 'seq'), may hold values from -0.125 to 0.125
- residual: bfloat16 [1152, 3584], P(('seq', 'heads')), may hold values from -2 to 2
- norm_gain: float32 [3584], replicated, may hold values from 0.25 to 1.75
- span_table: int32 [32], replicated, may hold values from 0 to 31, each once
Outputs:
- new_residual: bfloat16 [1152, 3584], P(('seq', 'heads'))
- normed: bfloat16 [1152, 3584], P(('seq', 'heads'))
Inputs may be any that keep to these rules, and one draw needn't show every extreme that they name: `span_table`: A permutation of the span numbers.
All inputs are finite; a program needn't handle non-finite values.
Results may differ from a plain program's by a relative error of at most 0.014.
Values may be sent and summed in bfloat16 or wider, within the bound.
No kernel may reach another device: no remote copies, remote signals or barrier semaphores. Data moves between devices by JAX's collectives and lax.ppermute only.
A program may use at most 128 MiB of HBM per device.

v0:
```python
import jax
import jax.numpy as jnp
from jax import lax
from jax.sharding import PartitionSpec as P

score_scale = 192.0 ** (-0.5)


def place_rows(start, count, span_len, span_table):
    index = start + jnp.arange(count, dtype=jnp.int32)
    which = index // span_len
    picked = jnp.where(
        which[:, None] == jnp.arange(span_table.shape[0], dtype=jnp.int32)[None, :],
        span_table[None, :],
        0,
    )
    return jnp.sum(picked, axis=1) * span_len + index % span_len


def per_device(
    q_nope,
    q_rope,
    latent,
    key_rope,
    absorb_key,
    absorb_value,
    w_out,
    residual,
    norm_gain,
    span_table,
):
    tok_rows = q_nope.shape[0]
    span_len = tok_rows // 2
    seq_count = lax.axis_size("seq")
    my_start = lax.axis_index("seq") * tok_rows
    query_pos = place_rows(my_start, tok_rows, span_len, span_table)
    q_lat = jnp.einsum(
        "thd,hdl->htl", q_nope, absorb_key, preferred_element_type=jnp.float32
    ).astype(jnp.bfloat16)
    rotary = jnp.transpose(q_rope, (1, 0, 2))
    local_heads = q_lat.shape[0]

    def attend(carry, pieces, start):
        top, total, summed = carry
        lat_piece, rope_piece = pieces
        key_pos = place_rows(start, lat_piece.shape[0], span_len, span_table)
        score = jnp.einsum("htl,nl->htn", q_lat, lat_piece, preferred_element_type=jnp.float32)
        score = (
            score
            + jnp.einsum("htr,nr->htn", rotary, rope_piece, preferred_element_type=jnp.float32)
        ) * score_scale
        seen = (key_pos[None, :] <= query_pos[:, None])[None, :, :]
        score = jnp.where(seen, score, jnp.float32(-1e30))
        fresh = jnp.maximum(top, jnp.max(score, axis=2))
        weight = jnp.where(seen, jnp.exp(score - fresh[:, :, None]), jnp.float32(0.0))
        factor = jnp.exp(top - fresh)
        total = total * factor + jnp.sum(weight, axis=2)
        summed = summed * factor[:, :, None] + jnp.einsum(
            "htn,nl->htl",
            weight.astype(jnp.bfloat16),
            lat_piece,
            preferred_element_type=jnp.float32,
        )
        return (fresh, total, summed)

    start_carry = (
        jnp.full((local_heads, tok_rows), -1e30, jnp.float32),
        jnp.zeros((local_heads, tok_rows), jnp.float32),
        jnp.zeros((local_heads, tok_rows, latent.shape[1]), jnp.float32),
    )
    all_lat, all_rope = (
        lax.all_gather(latent, "seq", axis=0, tiled=True),
        lax.all_gather(key_rope, "seq", axis=0, tiled=True),
    )
    block = tok_rows * min(8, seq_count)
    steps_count = all_lat.shape[0] // block

    def visit(step, carry):
        begin = (step * block).astype(jnp.int32)
        lat_piece = lax.dynamic_slice_in_dim(all_lat, begin, block, 0)
        rope_piece = lax.dynamic_slice_in_dim(all_rope, begin, block, 0)
        return attend(carry, (lat_piece, rope_piece), begin)

    top, total, summed = lax.fori_loop(0, steps_count, visit, start_carry)
    context = (summed / total[:, :, None]).astype(jnp.bfloat16)
    per_head = jnp.einsum(
        "htl,hle->the", context, absorb_value, preferred_element_type=jnp.float32
    ).astype(jnp.bfloat16)
    heads_out = per_head.reshape(tok_rows, local_heads * per_head.shape[2])
    every_row = lax.all_gather(heads_out, "seq", axis=0, tiled=True)
    columns = jnp.dot(every_row, w_out, preferred_element_type=jnp.float32).astype(jnp.bfloat16)
    partial_value = lax.all_to_all(columns, "seq", split_axis=0, concat_axis=1, tiled=True).astype(
        jnp.float32
    )
    projected = lax.psum_scatter(
        partial_value.astype(jnp.bfloat16), "heads", scatter_dimension=0, tiled=True
    ).astype(jnp.float32)
    hidden = residual.astype(jnp.float32) + projected
    new_residual = hidden.astype(jnp.bfloat16)
    scale = lax.rsqrt(jnp.mean(hidden * hidden, axis=1, keepdims=True) + 1e-06)
    normed = (hidden * scale * norm_gain[None, :]).astype(jnp.bfloat16)
    return (new_residual, normed)


def solution(mesh):
    in_specs = (
        P("seq", "heads", None),
        P("seq", "heads", None),
        P("seq", None),
        P("seq", None),
        P("heads", None, None),
        P("heads", None, None),
        P("heads", "seq"),
        P(("seq", "heads"), None),
        P(),
        P(),
    )
    out_specs = (P(("seq", "heads"), None), P(("seq", "heads"), None))
    return jax.shard_map(
        per_device, mesh=mesh, in_specs=in_specs, out_specs=out_specs, check_vma=False
    )
```

profile of v0, /device:TPU:0, one launch (start us, length us, event | category | flops | bytes accessed | tf_op | source)
XLA Modules:
  0.0 225.6 jit_solution(14816708200302043049)
XLA Ops:
  7.2 0.0 copy-start
  7.2 0.0 copy-start.6
  7.2 0.0 all-gather.4.cloned.1.call-start
  7.2 0.7 all-gather.4.cloned.1.call-update
  7.9 0.0 all-gather.6.cloned.1.call-start
  8.0 24.1 %all-gather = bf16[16,72,64]{1,2,0:T(8,128)(2,1)S(1)} all-gather(bf16[1,72,64]{1,2,0:T(8,128)(2,1)} %bitcast.47), channel_id=1, replica_groups=mesh['heads'=2,'seq'=16] {'seq'}, dimensions={0}, use_global_device_ids=true | all-gather | bytes 156672 | tf_op jit(solution)/shard_map/all_gather | solution.py:73
  32.1 0.2 copy.34
  32.3 0.3 reshape.96
  32.6 0.7 select_reduce_fusion.1
  33.4 4.7 %convolution_convert_fusion.1 = bf16[32,72,512]{2,1,0:T(8,128)(2,1)} fusion(bf16[32,128,512]{2,1,0:T(8,128)(2,1)} %param.16, bf16[72,32,128]{2,1,0:T(8,128)(2,1)} %param.12), kind=kOutput, calls=%fused_computation.41 | convolution fusion | flops 303169536 | bytes 7143424 | tf_op jit(solution)/shard_map/thd,hdl->htl/dot_general | solution.py:37
  38.0 13.4 %all-gather.4.cloned.1.call-done = bf16[1152,512]{1,0:T(8,128)(2,1)} async-done(((bf16[72,512]{1,0:T(8,128)(2,1)}), bf16[1152,512]{1,0:T(8,128)(2,1)}) %all-gather.4.cloned.1.call-update) | async-done | bytes 1179664 | tf_op jit(solution)/shard_map/all_gather | solution.py:72
  51.4 0.0 copy-done.6
  51.4 36.1 %while.20 = (s32[]{:T(128)}, f32[32,72]{1,0:T(8,128)S(1)}, f32[32,72]{1,0:T(8,128)S(1)}, f32[32,72,512]{2,1,0:T(8,128)}, s32[32]{0:T(128)S(1)}, /*index=5*/s32[7...) while((s32[]{:T(128)}, f32[32,72]{1,0:T(8,128)S(1)}, ...), condition=%wide.region_5.6_spmd.clone, body=%wide.region_1.5_spmd.clone.sunk | while | flops 2904706304 | bytes 68787400 | solution.py:84
  51.4 0.0 copy-start.3
  51.4 3.9 %fusion.59 = f32[576,32,72]{0,2,1:T(8,128)S(1)} fusion(bf16[32,72,512]{2,1,0:T(8,128)(2,1)} %get-tuple-element.413, bf16[1152,512]{1,0:T(8,128)(2,1)} %get-tuple-element.412, s32[]{:T(128)S(6)} %select_n.141), kind=kOutput, calls=%fused_computation.11.clone.1 | convolution fusion | flops 1358954496 | bytes 8257540 | tf_op jit(solution)/shard_map/while/body/eval_jaxpr/htl,nl->htn/dot_general | solution.py:47
  55.4 0.1 select_reduce_fusion.3
  55.5 0.1 broadcast_compare_fusion.2
  55.6 0.0 copy-done.3
  55.6 0.0 copy-start.2
  55.6 4.2 %fusion.61 = (f32[32,72]{1,0:T(8,128)S(1)}, f32[32,72,576]{2,1,0:T(8,128)}) fusion(f32[576,32,72]{0,2,1:T(8,128)S(1)} %fusion.59, bf16[32,72,64]{1,2,0:T(8,128)(2,1)S(1)} %copy-done.3, bf16[1152,64]{0,1:T(8,128)(2,1)S(1)} %get-tuple-element.414, s32[]{:T(128)S(6)} %select_n.141, pred[72,576]{1,0:T(8,128)(4,1)S(1)} %broadcast_compare_fusion.2), kind=kOutput, calls=%fused_computation.58.clone.1 | convolution fusion | flops 175175424 | bytes 11868164 | tf_op jit(solution)/shard_map/while/body/eval_jaxpr/htr,nr->htn/dot_general | solution.py:50
  59.8 0.0 copy-start.1
  59.9 4.1 %fusion.62 = f32[32,72]{1,0:T(8,128)S(1)} fusion(f32[32,72,576]{2,1,0:T(8,128)} %get-tuple-element.375, f32[32,72]{1,0:T(8,128)S(1)} %select_maximum_fusion.2, pred[72,576]{1,0:T(8,128)(4,1)S(1)} %broadcast_compare_fusion.2), kind=kLoop, calls=%fused_computation.3.clone.1 | loop fusion | flops 3979008 | bytes 5368320 | tf_op jit(solution)/shard_map/while/body/eval_jaxpr/reduce_sum | solution.py:57
  64.0 0.0 copy-done.2
  64.0 0.3 copy-done.1
  64.3 4.4 %fusion.64 = f32[32,72,512]{2,1,0:T(8,128)} fusion(f32[32,72,512]{2,1,0:T(8,128)} %get-tuple-element.395, f32[32,72]{1,0:T(8,128)S(1)} %get-tuple-element.377, pred[]{:T(512)S(6)} %compare.3, f32[32,72,576]{2,1,0:T(8,128)S(1)} %copy-done.1, f32[32,72]{1,0:T(8,128)S(1)} %select_maximum_fusion.2, pred[72,576]{1,0:T(8,128)(4,1)S(1)} %broadcast_compare_fusion.2, ...), kind=kOutput, calls=%fused_computation.5.clone.1 | convolution fusion | flops 1366474752 | bytes 16004101 | tf_op jit(solution)/shard_map/while/body/eval_jaxpr/htn,nl->htl/dot_general | solution.py:58
  68.6 0.0 copy-start.3
  68.6 3.9 %fusion.59 = f32[576,32,72]{0,2,1:T(8,128)S(1)} fusion(bf16[32,72,512]{2,1,0:T(8,128)(2,1)} %get-tuple-element.413, bf16[1152,512]{1,0:T(8,128)(2,1)} %get-tuple-element.412, s32[]{:T(128)S(6)} %select_n.141), kind=kOutput, calls=%fused_computation.11.clone.1 | convolution fusion | flops 1358954496 | bytes 8257540 | tf_op jit(solution)/shard_map/while/body/eval_jaxpr/htl,nl->htn/dot_general | solution.py:47
  72.6 0.1 select_reduce_fusion.3
  72.7 0.1 broadcast_compare_fusion.2
  72.8 0.0 copy-done.3
  72.8 0.0 copy-start.2
  72.8 4.2 %fusion.61 = (f32[32,72]{1,0:T(8,128)S(1)}, f32[32,72,576]{2,1,0:T(8,128)}) fusion(f32[576,32,72]{0,2,1:T(8,128)S(1)} %fusion.59, bf16[32,72,64]{1,2,0:T(8,128)(2,1)S(1)} %copy-done.3, bf16[1152,64]{0,1:T(8,128)(2,1)S(1)} %get-tuple-element.414, s32[]{:T(128)S(6)} %select_n.141, pred[72,576]{1,0:T(8,128)(4,1)S(1)} %broadcast_compare_fusion.2), kind=kOutput, calls=%fused_computation.58.clone.1 | convolution fusion | flops 175175424 | bytes 11868164 | tf_op jit(solution)/shard_map/while/body/eval_jaxpr/htr,nr->htn/dot_general | solution.py:50
  77.1 0.0 copy-start.1
  77.1 4.1 %fusion.62 = f32[32,72]{1,0:T(8,128)S(1)} fusion(f32[32,72,576]{2,1,0:T(8,128)} %get-tuple-element.375, f32[32,72]{1,0:T(8,128)S(1)} %select_maximum_fusion.2, pred[72,576]{1,0:T(8,128)(4,1)S(1)} %broadcast_compare_fusion.2), kind=kLoop, calls=%fused_computation.3.clone.1 | loop fusion | flops 3979008 | bytes 5368320 | tf_op jit(solution)/shard_map/while/body/eval_jaxpr/reduce_sum | solution.py:57
  81.2 0.0 copy-done.2
  81.2 0.3 copy-done.1
  81.5 6.0 %fusion.64 = f32[32,72,512]{2,1,0:T(8,128)} fusion(f32[32,72,512]{2,1,0:T(8,128)} %get-tuple-element.395, f32[32,72]{1,0:T(8,128)S(1)} %get-tuple-element.377, pred[]{:T(512)S(6)} %compare.3, f32[32,72,576]{2,1,0:T(8,128)S(1)} %copy-done.1, f32[32,72]{1,0:T(8,128)S(1)} %select_maximum_fusion.2, pred[72,576]{1,0:T(8,128)(4,1)S(1)} %broadcast_compare_fusion.2, ...), kind=kOutput, calls=%fused_computation.5.clone.1 | convolution fusion | flops 1366474752 | bytes 16004101 | tf_op jit(solution)/shard_map/while/body/eval_jaxpr/htn,nl->htl/dot_general | solution.py:58
  87.5 4.6 %fusion.31 = bf16[32,9,8,128]{3,2,1,0:T(8,128)(2,1)S(1)} fusion(bf16[32,512,128]{2,1,0:T(8,128)(2,1)} %param.17, f32[32,72,512]{2,1,0:T(8,128)} %get-tuple-element.248, f32[32,72]{1,0:T(8,128)S(1)} %get-tuple-element.249), kind=kOutput, calls=%fused_computation.43 | convolution fusion | flops 304644096 | bytes 9511936 | tf_op jit(solution)/shard_map/htl,hle->the/dot_general | solution.py:86
  92.1 0.9 copy.42
  93.1 0.0 all-gather.6.cloned.1.call-update
  93.1 79.9 %all-gather.6.cloned.1.call-done = bf16[1152,4096]{1,0:T(8,128)(2,1)} async-done(((bf16[72,4096]{1,0:T(8,128)(2,1)}), bf16[1152,4096]{1,0:T(8,128)(2,1)}) %all-gather.6.cloned.1.call-update) | async-done | bytes 9437200 | tf_op jit(solution)/shard_map/all_gather | solution.py:90
  173.0 0.0 copy-done
  173.0 6.7 %convolution_convert_fusion = bf16[1152,224]{0,1:T(8,128)(2,1)S(1)} fusion(bf16[1152,4096]{1,0:T(8,128)(2,1)} %all-gather.6.cloned.1.call-done, bf16[4096,224]{0,1:T(8,128)(2,1)S(1)} %copy-done), kind=kOutput, calls=%fused_computation.39 | convolution fusion | flops 2114187264 | bytes 11788288 | tf_op jit(solution)/shard_map/dot_general | solution.py:91
  179.8 0.0 copy-start.7
  179.8 0.0 copy-start.4
  179.8 0.0 copy-start.5
  179.8 0.2 copy.36
  180.0 20.2 %all_to_all.19 = bf16[16,72,224]{2,1,0:T(8,128)(2,1)S(1)} all-to-all(bf16[16,72,224]{2,1,0:T(8,128)(2,1)S(1)} %bitcast.45), channel_id=1, replica_groups=mesh['heads'=2,'seq'=16] {'seq'}, dimensions={0} | all-to-all | bytes 1032192 | tf_op jit(solution)/shard_map/all_to_all | solution.py:92
  200.2 0.1 copy.37
  200.3 1.0 all_to_all.17
  201.3 11.8 %fusion = bf16[40,3584]{1,0:T(8,128)(2,1)S(1)} fusion(bf16[72,3584]{1,0:T(8,128)(2,1)S(1)} %all_to_all.17), kind=kCustom, calls=%all-reduce-scatter | all-reduce-scatter fusion | flops 286721 | bytes 803328
  213.1 2.5 %collective-permute-start = (bf16[4,3584]{1,0:T(4,128)(2,1)S(1)}, bf16[4,3584]{1,0:T(4,128)(2,1)S(1)}, u32[]{:S(2)}, u32[]{:S(2)}) collective-permute-start(bf16[4,3584]{1,0:T(4,128)(2,1)S(1)} %slice), channel_id=1, source_target_pairs={{0,16},{1,17},{2,18},{3,19},{4,20},{5,21},{6,22},{7,23},{8,24},{9,... | collective-permute-start | bytes 86024
  215.6 0.0 copy-done.7
  215.6 0.6 dynamic-slice.4
  216.8 0.3 collective-permute-done
  217.1 0.4 concatenate
  217.5 0.0 copy-done.4
  217.5 0.2 multiply_reduce_fusion
  217.8 0.0 copy-done.5
  217.8 1.0 multiply_convert_fusion
  (17 shorter events, 0.2 us)
Async XLA Ops:
  7.2 165.8 %copy-start = (bf16[4096,224]{0,1:T(8,128)(2,1)S(1)}, bf16[4096,224]{0,1:T(8,128)(2,1)}, u32[]{:S(2)}) copy-start(bf16[4096,224]{0,1:T(8,128)(2,1)} %param.18) | copy-start | bytes 5505028
  7.2 44.2 %copy-start.6 = (s32[32]{0:T(128)S(1)}, s32[32]{0:T(128)}, u32[]{:S(2)}) copy-start(s32[32]{0:T(128)} %param.21) | copy-start | bytes 388
  7.2 44.2 %all-gather.4.cloned.1.call-start = ((), (), s32[]{:S(2)}) async-start(), calls=%async_computation.1 | async-start | bytes 1253376 | tf_op jit(solution)/shard_map/all_gather | solution.py:72
  7.9 165.1 %all-gather.6.cloned.1.call-start = ((), (), s32[]{:S(2)}) async-start(), calls=%async_computation.2 | async-start | bytes 10027008 | tf_op jit(solution)/shard_map/all_gather | solution.py:90
  51.4 4.2 %copy-start.3 = (bf16[32,72,64]{1,2,0:T(8,128)(2,1)S(1)}, bf16[32,72,64]{1,2,0:T(8,128)(2,1)}, u32[]{:S(2)}) copy-start(bf16[32,72,64]{1,2,0:T(8,128)(2,1)} %get-tuple-element.415) | copy-start | bytes 884740 | tf_op jit(solution)/shard_map/while
  55.6 8.4 %copy-start.2 = (bf16[1152,512]{1,0:T(8,128)(2,1)S(1)}, bf16[1152,512]{1,0:T(8,128)(2,1)}, u32[]{:S(2)}) copy-start(bf16[1152,512]{1,0:T(8,128)(2,1)} %get-tuple-element.412) | copy-start | bytes 3538948 | tf_op jit(solution)/shard_map/while
  59.8 4.4 %copy-start.1 = (f32[32,72,576]{2,1,0:T(8,128)S(1)}, f32[32,72,576]{2,1,0:T(8,128)}, u32[]{:S(2)}) copy-start(f32[32,72,576]{2,1,0:T(8,128)} %get-tuple-element.375) | copy-start | bytes 15925252 | tf_op jit(solution)/shard_map/while
  68.6 4.2 %copy-start.3 = (bf16[32,72,64]{1,2,0:T(8,128)(2,1)S(1)}, bf16[32,72,64]{1,2,0:T(8,128)(2,1)}, u32[]{:S(2)}) copy-start(bf16[32,72,64]{1,2,0:T(8,128)(2,1)} %get-tuple-element.415) | copy-start | bytes 884740 | tf_op jit(solution)/shard_map/while
  72.8 8.4 %copy-start.2 = (bf16[1152,512]{1,0:T(8,128)(2,1)S(1)}, bf16[1152,512]{1,0:T(8,128)(2,1)}, u32[]{:S(2)}) copy-start(bf16[1152,512]{1,0:T(8,128)(2,1)} %get-tuple-element.412) | copy-start | bytes 3538948 | tf_op jit(solution)/shard_map/while
  77.1 4.4 %copy-start.1 = (f32[32,72,576]{2,1,0:T(8,128)S(1)}, f32[32,72,576]{2,1,0:T(8,128)}, u32[]{:S(2)}) copy-start(f32[32,72,576]{2,1,0:T(8,128)} %get-tuple-element.375) | copy-start | bytes 15925252 | tf_op jit(solution)/shard_map/while
  179.8 35.8 %copy-start.7 = (u32[32]{0:T(128)S(1)}, u32[32]{0:T(128)}, u32[]{:S(2)}) copy-start(u32[32]{0:T(128)} %constant.152) | copy-start | bytes 388
  179.8 37.8 %copy-start.4 = (bf16[36,3584]{1,0:T(8,128)(2,1)S(1)}, bf16[36,3584]{1,0:T(8,128)(2,1)}, u32[]{:S(2)}) copy-start(bf16[36,3584]{1,0:T(8,128)(2,1)} %param.19) | copy-start | bytes 774148
  179.8 38.0 %copy-start.5 = (f32[3584]{0:T(1024)S(1)}, f32[3584]{0:T(1024)}, u32[]{:S(2)}) copy-start(f32[3584]{0:T(1024)} %param.20) | copy-start | bytes 43012
  213.1 4.0 %collective-permute-start = (bf16[4,3584]{1,0:T(4,128)(2,1)S(1)}, bf16[4,3584]{1,0:T(4,128)(2,1)S(1)}, u32[]{:S(2)}, u32[]{:S(2)}) collective-permute-start(bf16[4,3584]{1,0:T(4,128)(2,1)S(1)} %slice), channel_id=1, source_target_pairs={{0,16},{1,17},{2,18},{3,19},{4,20},{5,21},{6,22},{7,23},{8,24},{9,... | collective-permute-start | bytes 86024
Sparse Core Ops, SparseCore 0:
  10.3 41.0 all-gather.3
  93.2 79.7 all-gather.5
where the time goes:
time: 226 us
  waiting for transfers between devices  94.3 us (42%)
  blocking collectives  56.1 us (25%)
  matrix products  42.8 us (19%)
  between operations  14.9 us (7%)
  other arithmetic  10.7 us (5%)
  local copies, waits for them, and re-layouts  4.29 us (2%)
  starting transfers between devices  2.54 us (1%)
    all_gather x1, waiting for transfers between devices, per_device(): every_row = lax.all_gather(heads_out, 'seq', axis=0, tiled=True)  79.9 us
    all_gather x1, blocking collectives, per_device(): lax.all_gather(key_rope, 'seq', axis=0, tiled=True)  24.1 us
    all_to_all x1, blocking collectives, per_device(): lax.all_to_all(columns, 'seq', split_axis=0, concat_axis=1, tiled=True)  20.2 us
    all_gather x1, waiting for transfers between devices, per_device(): lax.all_gather(latent, 'seq', axis=0, tiled=True)  13.4 us
    unnamed x1, blocking collectives  11.8 us
    dot_general x2, matrix products, attend(): jnp.einsum('htn,nl->htl', weight.astype(jnp.bfloat16), lat_piece, preferr...  10.4 us
    dot_general x2, matrix products, attend(): jnp.einsum('htr,nr->htn', rotary, rope_piece, preferred_element_type=jnp....  8.46 us
    reduce_sum x2, other arithmetic, attend(): total = total * factor + jnp.sum(weight, axis=2)  8.21 us
  transfers between devices with their start and end apart: 3, of which 3 were waited for; matrix products, arithmetic and copies ran while one was open for 3% of the time, Pallas kernels for 0%

commit v1 on v0

--- a/solution.py
+++ b/solution.py
@@ -4,6 +4,12 @@
 from jax.sharding import PartitionSpec as P
 
 score_scale = 192.0 ** (-0.5)
+
+
+def move_loops(page):
+    f_now = jnp.stack([page] * lax.axis_size("seq"))
+    v_now = lax.all_to_all(f_now, "seq", 0, 0)
+    return jnp.concatenate(v_now, axis=0)
 
 
 def place_rows(start, count, span_len, span_table):
@@ -68,10 +74,7 @@
         jnp.zeros((local_heads, tok_rows), jnp.float32),
         jnp.zeros((local_heads, tok_rows, latent.shape[1]), jnp.float32),
     )
-    all_lat, all_rope = (
-        lax.all_gather(latent, "seq", axis=0, tiled=True),
-        lax.all_gather(key_rope, "seq", axis=0, tiled=True),
-    )
+    all_lat, all_rope = (lax.all_gather(latent, "seq", axis=0, tiled=True), move_loops(key_rope))
     block = tok_rows * min(8, seq_count)
     steps_count = all_lat.shape[0] // block
 

time: 226 us -> 227 us (level)
  blocking collectives: 56.1 us -> 31.9 us
  waiting for transfers between devices: 94.3 us -> 111 us
  starting transfers between devices: 2.54 us -> 9.96 us
    all_gather x1 -> x0, blocking collectives: 24.1 us -> none  [per_device(): lax.all_gather(key_rope, 'seq', axis=0, tiled=True)]
    all_gather x1, waiting for transfers between devices: 13.4 us -> 24.1 us  [per_device(): lax.all_gather(latent, 'seq', axis=0, tiled=True)]
    all_to_all x0 -> x1, starting transfers between devices: none -> 7.41 us  [move_loops(): v_now = lax.all_to_all(f_now, 'seq', 0, 0)]
    all_to_all x0 -> x1, waiting for transfers between devices: none -> 5.84 us  [move_loops(): v_now = lax.all_to_all(f_now, 'seq', 0, 0)]
  transfers between devices with their start and end apart: 3 -> 4, of which waited for: 3 -> 4; matrix products, arithmetic and copies ran while one was open for 3% -> 3% of each run, Pallas kernels for 0% -> 0%
where the time goes in v1:
time: 227 us; the launch traced here: 226 us
  waiting for transfers between devices  111 us (49%)
  matrix products  42.8 us (19%)
  blocking collectives  31.9 us (14%)
  between operations  14.9 us (7%)
  starting transfers between devices  9.96 us (4%)
  other arithmetic  9.94 us (4%)
  local copies, waits for them, and re-layouts  5.84 us (3%)
    all_gather x1, waiting for transfers between devices, per_device(): every_row = lax.all_gather(heads_out, 'seq', axis=0, tiled=True)  79.9 us
    all_gather x1, waiting for transfers between devices, per_device(): lax.all_gather(latent, 'seq', axis=0, tiled=True)  24.1 us
    all_to_all x1, blocking collectives, per_device(): lax.all_to_all(columns, 'seq', split_axis=0, concat_axis=1, tiled=True)  20.2 us
    unnamed x1, blocking collectives  11.8 us
    dot_general x2, matrix products, attend(): jnp.einsum('htn,nl->htl', weight.astype(jnp.bfloat16), lat_piece, preferr...  10.4 us
    dot_general x2, matrix products, attend(): jnp.einsum('htr,nr->htn', rotary, rope_piece, preferred_element_type=jnp....  8.48 us
    reduce_sum x2, other arithmetic, attend(): total = total * factor + jnp.sum(weight, axis=2)  8.14 us
    dot_general x2, matrix products, attend(): jnp.einsum('htl,nl->htn', q_lat, lat_piece, preferred_element_type=jnp.fl...  7.9 us
  transfers between devices with their start and end apart: 4, of which 4 were waited for; matrix products, arithmetic and copies ran while one was open for 3% of the time, Pallas kernels for 0%

profile of v1, /device:TPU:0, one launch (start us, length us, event | category | flops | bytes accessed | tf_op | source)
XLA Modules:
  0.0 226.3 jit_solution(7772394258128054134)
XLA Ops:
  7.2 0.0 copy-start
  7.2 0.0 copy-start.6
  7.2 0.0 all-gather.3.cloned.1.call-start
  7.2 0.7 all-gather.3.cloned.1.call-update
  7.9 1.5 stack.2
  9.4 7.4 %all-to-all-start = ((bf16[16,72,64]{1,2,0:T(8,128)(2,1)}), bf16[16,72,64]{1,2,0:T(8,128)(2,1)S(1)}, u32[]{:S(2)}, u32[]{:S(2)}) async-start(bf16[16,72,64]{1,2,0:T(8,128)(2,1)} %stack.2), calls=%async_computation | async-start | bytes 524288 | tf_op jit(solution)/shard_map/all_to_all | solution.py:11
  16.8 0.0 all-gather.5.cloned.1.call-start
  16.9 4.7 %convolution_convert_fusion.1 = bf16[32,72,512]{2,1,0:T(8,128)(2,1)} fusion(bf16[32,128,512]{2,1,0:T(8,128)(2,1)} %param.16, bf16[72,32,128]{2,1,0:T(8,128)(2,1)} %param.12), kind=kOutput, calls=%fused_computation.41 | convolution fusion | flops 303169536 | bytes 7143424 | tf_op jit(solution)/shard_map/thd,hdl->htl/dot_general | solution.py:43
  21.5 0.0 copy-done.6
  21.5 0.1 select_reduce_fusion.1
  21.7 5.8 %all-to-all-done = bf16[16,72,64]{1,2,0:T(8,128)(2,1)S(1)} async-done(((bf16[16,72,64]{1,2,0:T(8,128)(2,1)}), bf16[16,72,64]{1,2,0:T(8,128)(2,1)S(1)}, u32[]{:S(2)}, u32[]{:S(2)}) %all-to-all-start) | async-done | bytes 147488 | tf_op jit(solution)/shard_map/all_to_all | solution.py:11
  27.5 0.2 copy.31
  27.7 0.3 reshape.99
  28.0 24.1 %all-gather.3.cloned.1.call-done = bf16[1152,512]{1,0:T(8,128)(2,1)} async-done(((bf16[72,512]{1,0:T(8,128)(2,1)}), bf16[1152,512]{1,0:T(8,128)(2,1)}) %all-gather.3.cloned.1.call-update) | async-done | bytes 1179664 | tf_op jit(solution)/shard_map/all_gather | solution.py:77
  52.1 36.1 %while.20 = (s32[]{:T(128)}, f32[32,72]{1,0:T(8,128)S(1)}, f32[32,72]{1,0:T(8,128)S(1)}, f32[32,72,512]{2,1,0:T(8,128)}, s32[32]{0:T(128)S(1)}, /*index=5*/s32[7...) while((s32[]{:T(128)}, f32[32,72]{1,0:T(8,128)S(1)}, ...), condition=%wide.region_5.6_spmd.clone, body=%wide.region_1.5_spmd.clone.sunk | while | flops 2904706304 | bytes 68787400 | solution.py:87
  52.1 0.0 copy-start.3
  52.1 3.9 %fusion.59 = f32[576,32,72]{0,2,1:T(8,128)S(1)} fusion(bf16[32,72,512]{2,1,0:T(8,128)(2,1)} %get-tuple-element.413, bf16[1152,512]{1,0:T(8,128)(2,1)} %get-tuple-element.412, s32[]{:T(128)S(6)} %select_n.141), kind=kOutput, calls=%fused_computation.11.clone.1 | convolution fusion | flops 1358954496 | bytes 8257540 | tf_op jit(solution)/shard_map/while/body/eval_jaxpr/htl,nl->htn/dot_general | solution.py:53
  56.1 0.1 select_reduce_fusion.3
  56.2 0.1 broadcast_compare_fusion.2
  56.3 0.0 copy-done.3
  56.3 0.0 copy-start.2
  56.3 4.2 %fusion.61 = (f32[32,72]{1,0:T(8,128)S(1)}, f32[32,72,576]{2,1,0:T(8,128)}) fusion(f32[576,32,72]{0,2,1:T(8,128)S(1)} %fusion.59, bf16[32,72,64]{1,2,0:T(8,128)(2,1)S(1)} %copy-done.3, bf16[1152,64]{0,1:T(8,128)(2,1)S(1)} %get-tuple-element.414, s32[]{:T(128)S(6)} %select_n.141, pred[72,576]{1,0:T(8,128)(4,1)S(1)} %broadcast_compare_fusion.2), kind=kOutput, calls=%fused_computation.58.clone.1 | convolution fusion | flops 175175424 | bytes 11868164 | tf_op jit(solution)/shard_map/while/body/eval_jaxpr/htr,nr->htn/dot_general | solution.py:56
  60.5 0.0 copy-start.1
  60.5 4.1 %fusion.62 = f32[32,72]{1,0:T(8,128)S(1)} fusion(f32[32,72,576]{2,1,0:T(8,128)} %get-tuple-element.375, f32[32,72]{1,0:T(8,128)S(1)} %select_maximum_fusion.2, pred[72,576]{1,0:T(8,128)(4,1)S(1)} %broadcast_compare_fusion.2), kind=kLoop, calls=%fused_computation.3.clone.1 | loop fusion | flops 3979008 | bytes 5368320 | tf_op jit(solution)/shard_map/while/body/eval_jaxpr/reduce_sum | solution.py:63
  64.6 0.0 copy-done.2
  64.6 0.3 copy-done.1
  64.9 4.4 %fusion.64 = f32[32,72,512]{2,1,0:T(8,128)} fusion(f32[32,72,512]{2,1,0:T(8,128)} %get-tuple-element.395, f32[32,72]{1,0:T(8,128)S(1)} %get-tuple-element.377, pred[]{:T(512)S(6)} %compare.3, f32[32,72,576]{2,1,0:T(8,128)S(1)} %copy-done.1, f32[32,72]{1,0:T(8,128)S(1)} %select_maximum_fusion.2, pred[72,576]{1,0:T(8,128)(4,1)S(1)} %broadcast_compare_fusion.2, ...), kind=kOutput, calls=%fused_computation.5.clone.1 | convolution fusion | flops 1366474752 | bytes 16004101 | tf_op jit(solution)/shard_map/while/body/eval_jaxpr/htn,nl->htl/dot_general | solution.py:64
  69.3 0.0 copy-start.3
  69.3 3.9 %fusion.59 = f32[576,32,72]{0,2,1:T(8,128)S(1)} fusion(bf16[32,72,512]{2,1,0:T(8,128)(2,1)} %get-tuple-element.413, bf16[1152,512]{1,0:T(8,128)(2,1)} %get-tuple-element.412, s32[]{:T(128)S(6)} %select_n.141), kind=kOutput, calls=%fused_computation.11.clone.1 | convolution fusion | flops 1358954496 | bytes 8257540 | tf_op jit(solution)/shard_map/while/body/eval_jaxpr/htl,nl->htn/dot_general | solution.py:53
  73.3 0.1 select_reduce_fusion.3
  73.4 0.1 broadcast_compare_fusion.2
  73.5 0.0 copy-done.3
  73.5 0.0 copy-start.2
  73.5 4.2 %fusion.61 = (f32[32,72]{1,0:T(8,128)S(1)}, f32[32,72,576]{2,1,0:T(8,128)}) fusion(f32[576,32,72]{0,2,1:T(8,128)S(1)} %fusion.59, bf16[32,72,64]{1,2,0:T(8,128)(2,1)S(1)} %copy-done.3, bf16[1152,64]{0,1:T(8,128)(2,1)S(1)} %get-tuple-element.414, s32[]{:T(128)S(6)} %select_n.141, pred[72,576]{1,0:T(8,128)(4,1)S(1)} %broadcast_compare_fusion.2), kind=kOutput, calls=%fused_computation.58.clone.1 | convolution fusion | flops 175175424 | bytes 11868164 | tf_op jit(solution)/shard_map/while/body/eval_jaxpr/htr,nr->htn/dot_general | solution.py:56
  77.8 0.0 copy-start.1
  77.8 4.1 %fusion.62 = f32[32,72]{1,0:T(8,128)S(1)} fusion(f32[32,72,576]{2,1,0:T(8,128)} %get-tuple-element.375, f32[32,72]{1,0:T(8,128)S(1)} %select_maximum_fusion.2, pred[72,576]{1,0:T(8,128)(4,1)S(1)} %broadcast_compare_fusion.2), kind=kLoop, calls=%fused_computation.3.clone.1 | loop fusion | flops 3979008 | bytes 5368320 | tf_op jit(solution)/shard_map/while/body/eval_jaxpr/reduce_sum | solution.py:63
  81.9 0.0 copy-done.2
  81.9 0.3 copy-done.1
  82.2 6.0 %fusion.64 = f32[32,72,512]{2,1,0:T(8,128)} fusion(f32[32,72,512]{2,1,0:T(8,128)} %get-tuple-element.395, f32[32,72]{1,0:T(8,128)S(1)} %get-tuple-element.377, pred[]{:T(512)S(6)} %compare.3, f32[32,72,576]{2,1,0:T(8,128)S(1)} %copy-done.1, f32[32,72]{1,0:T(8,128)S(1)} %select_maximum_fusion.2, pred[72,576]{1,0:T(8,128)(4,1)S(1)} %broadcast_compare_fusion.2, ...), kind=kOutput, calls=%fused_computation.5.clone.1 | convolution fusion | flops 1366474752 | bytes 16004101 | tf_op jit(solution)/shard_map/while/body/eval_jaxpr/htn,nl->htl/dot_general | solution.py:64
  88.2 4.6 %fusion.31 = bf16[32,9,8,128]{3,2,1,0:T(8,128)(2,1)S(1)} fusion(bf16[32,512,128]{2,1,0:T(8,128)(2,1)} %param.17, f32[32,72,512]{2,1,0:T(8,128)} %get-tuple-element.248, f32[32,72]{1,0:T(8,128)S(1)} %get-tuple-element.249), kind=kOutput, calls=%fused_computation.43 | convolution fusion | flops 304644096 | bytes 9511936 | tf_op jit(solution)/shard_map/htl,hle->the/dot_general | solution.py:89
  92.8 0.9 copy.39
  93.8 0.0 all-gather.5.cloned.1.call-update
  93.8 79.9 %all-gather.5.cloned.1.call-done = bf16[1152,4096]{1,0:T(8,128)(2,1)} async-done(((bf16[72,4096]{1,0:T(8,128)(2,1)}), bf16[1152,4096]{1,0:T(8,128)(2,1)}) %all-gather.5.cloned.1.call-update) | async-done | bytes 9437200 | tf_op jit(solution)/shard_map/all_gather | solution.py:93
  173.7 0.0 copy-done
  173.7 6.7 %convolution_convert_fusion = bf16[1152,224]{0,1:T(8,128)(2,1)S(1)} fusion(bf16[1152,4096]{1,0:T(8,128)(2,1)} %all-gather.5.cloned.1.call-done, bf16[4096,224]{0,1:T(8,128)(2,1)S(1)} %copy-done), kind=kOutput, calls=%fused_computation.39 | convolution fusion | flops 2114187264 | bytes 11788288 | tf_op jit(solution)/shard_map/dot_general | solution.py:94
  180.5 0.0 copy-start.7
  180.5 0.0 copy-start.4
  180.5 0.0 copy-start.5
  180.5 0.2 copy.33
  180.8 20.2 %all_to_all.24 = bf16[16,72,224]{2,1,0:T(8,128)(2,1)S(1)} all-to-all(bf16[16,72,224]{2,1,0:T(8,128)(2,1)S(1)} %bitcast.44), channel_id=1, replica_groups=mesh['heads'=2,'seq'=16] {'seq'}, dimensions={0} | all-to-all | bytes 1032192 | tf_op jit(solution)/shard_map/all_to_all | solution.py:95
  200.9 0.1 copy.34
  201.0 1.0 all_to_all.21
  202.0 11.8 %fusion = bf16[40,3584]{1,0:T(8,128)(2,1)S(1)} fusion(bf16[72,3584]{1,0:T(8,128)(2,1)S(1)} %all_to_all.21), kind=kCustom, calls=%all-reduce-scatter | all-reduce-scatter fusion | flops 286721 | bytes 803328
  213.8 2.5 %collective-permute-start = (bf16[4,3584]{1,0:T(4,128)(2,1)S(1)}, bf16[4,3584]{1,0:T(4,128)(2,1)S(1)}, u32[]{:S(2)}, u32[]{:S(2)}) collective-permute-start(bf16[4,3584]{1,0:T(4,128)(2,1)S(1)} %slice), channel_id=1, source_target_pairs={{0,16},{1,17},{2,18},{3,19},{4,20},{5,21},{6,22},{7,23},{8,24},{9,... | collective-permute-start | bytes 86024
  216.3 0.0 copy-done.7
  216.3 0.6 dynamic-slice.4
  217.5 0.3 collective-permute-done
  217.8 0.4 concatenate
  218.2 0.0 copy-done.4
  218.3 0.2 multiply_reduce_fusion
  218.5 0.0 copy-done.5
  218.5 1.0 multiply_convert_fusion
  (17 shorter events, 0.2 us)
Async XLA Ops:
  7.2 166.6 %copy-start = (bf16[4096,224]{0,1:T(8,128)(2,1)S(1)}, bf16[4096,224]{0,1:T(8,128)(2,1)}, u32[]{:S(2)}) copy-start(bf16[4096,224]{0,1:T(8,128)(2,1)} %param.18) | copy-start | bytes 5505028
  7.2 14.4 %copy-start.6 = (s32[32]{0:T(128)S(1)}, s32[32]{0:T(128)}, u32[]{:S(2)}) copy-start(s32[32]{0:T(128)} %param.21) | copy-start | bytes 388
  7.2 44.9 %all-gather.3.cloned.1.call-start = ((), (), s32[]{:S(2)}) async-start(), calls=%async_computation.2 | async-start | bytes 1253376 | tf_op jit(solution)/shard_map/all_gather | solution.py:77
  9.4 18.1 %all-to-all-start = ((bf16[16,72,64]{1,2,0:T(8,128)(2,1)}), bf16[16,72,64]{1,2,0:T(8,128)(2,1)S(1)}, u32[]{:S(2)}, u32[]{:S(2)}) async-start(bf16[16,72,64]{1,2,0:T(8,128)(2,1)} %stack.2), calls=%async_computation | async-start | bytes 524288 | tf_op jit(solution)/shard_map/all_to_all | solution.py:11
  16.8 156.9 %all-gather.5.cloned.1.call-start = ((), (), s32[]{:S(2)}) async-start(), calls=%async_computation.3 | async-start | bytes 10027008 | tf_op jit(solution)/shard_map/all_gather | solution.py:93
  52.1 4.2 %copy-start.3 = (bf16[32,72,64]{1,2,0:T(8,128)(2,1)S(1)}, bf16[32,72,64]{1,2,0:T(8,128)(2,1)}, u32[]{:S(2)}) copy-start(bf16[32,72,64]{1,2,0:T(8,128)(2,1)} %get-tuple-element.415) | copy-start | bytes 884740 | tf_op jit(solution)/shard_map/while
  56.3 8.4 %copy-start.2 = (bf16[1152,512]{1,0:T(8,128)(2,1)S(1)}, bf16[1152,512]{1,0:T(8,128)(2,1)}, u32[]{:S(2)}) copy-start(bf16[1152,512]{1,0:T(8,128)(2,1)} %get-tuple-element.412) | copy-start | bytes 3538948 | tf_op jit(solution)/shard_map/while
  60.5 4.4 %copy-start.1 = (f32[32,72,576]{2,1,0:T(8,128)S(1)}, f32[32,72,576]{2,1,0:T(8,128)}, u32[]{:S(2)}) copy-start(f32[32,72,576]{2,1,0:T(8,128)} %get-tuple-element.375) | copy-start | bytes 15925252 | tf_op jit(solution)/shard_map/while
  69.3 4.2 %copy-start.3 = (bf16[32,72,64]{1,2,0:T(8,128)(2,1)S(1)}, bf16[32,72,64]{1,2,0:T(8,128)(2,1)}, u32[]{:S(2)}) copy-start(bf16[32,72,64]{1,2,0:T(8,128)(2,1)} %get-tuple-element.415) | copy-start | bytes 884740 | tf_op jit(solution)/shard_map/while
  73.5 8.4 %copy-start.2 = (bf16[1152,512]{1,0:T(8,128)(2,1)S(1)}, bf16[1152,512]{1,0:T(8,128)(2,1)}, u32[]{:S(2)}) copy-start(bf16[1152,512]{1,0:T(8,128)(2,1)} %get-tuple-element.412) | copy-start | bytes 3538948 | tf_op jit(solution)/shard_map/while
  77.8 4.4 %copy-start.1 = (f32[32,72,576]{2,1,0:T(8,128)S(1)}, f32[32,72,576]{2,1,0:T(8,128)}, u32[]{:S(2)}) copy-start(f32[32,72,576]{2,1,0:T(8,128)} %get-tuple-element.375) | copy-start | bytes 15925252 | tf_op jit(solution)/shard_map/while
  180.5 35.8 %copy-start.7 = (u32[32]{0:T(128)S(1)}, u32[32]{0:T(128)}, u32[]{:S(2)}) copy-start(u32[32]{0:T(128)} %constant.152) | copy-start | bytes 388
  180.5 37.8 %copy-start.4 = (bf16[36,3584]{1,0:T(8,128)(2,1)S(1)}, bf16[36,3584]{1,0:T(8,128)(2,1)}, u32[]{:S(2)}) copy-start(bf16[36,3584]{1,0:T(8,128)(2,1)} %param.19) | copy-start | bytes 774148
  180.5 38.0 %copy-start.5 = (f32[3584]{0:T(1024)S(1)}, f32[3584]{0:T(1024)}, u32[]{:S(2)}) copy-start(f32[3584]{0:T(1024)} %param.20) | copy-start | bytes 43012
  213.8 4.0 %collective-permute-start = (bf16[4,3584]{1,0:T(4,128)(2,1)S(1)}, bf16[4,3584]{1,0:T(4,128)(2,1)S(1)}, u32[]{:S(2)}, u32[]{:S(2)}) collective-permute-start(bf16[4,3584]{1,0:T(4,128)(2,1)S(1)} %slice), channel_id=1, source_target_pairs={{0,16},{1,17},{2,18},{3,19},{4,20},{5,21},{6,22},{7,23},{8,24},{9,... | collective-permute-start | bytes 86024
Sparse Core Ops, SparseCore 0:
  10.3 41.7 all-gather.2
  93.9 79.7 all-gather.4
